TPU v7x, 8 devices: a whole 2x2x1 slice. The times are simulated.
8 devices in a mesh: dp: 2 (over y, z), tp: 4 (over x, core).
Axes of the slice: x: 2, y: 2, z: 1, core: 2. Of those that a mesh axis runs over, the one named last changes fastest.
Arguments:
- x: bfloat16 [256, 4096], P('dp'), parts along dimension 0
- w_gate: bfloat16 [4096, 10240], P(None, 'tp')
- w_up: bfloat16 [4096, 10240], P(None, 'tp')
- w_down: bfloat16 [10240, 4096], P('tp')
Outputs:
- output: bfloat16 [256, 4096], P('dp'), parts along dimension 0
There are 2 independent parts. A program takes and returns all parts, laid end to end along the dimension named above; an argument that names none is the same for every part.
All inputs are finite; a program needn't handle non-finite values.
Results may differ from a plain program's by a relative error of at most 0.016.
Values are sent between devices in bfloat16 or wider.
A program may use at most 2 GiB of HBM per device.

v0:
```python
import jax
import jax.numpy as jnp
from jax import lax
from jax.sharding import PartitionSpec as P


def solution(mesh):
    def step(x, w_gate, w_up, w_down):
        gate = jnp.dot(x, w_gate, preferred_element_type=jnp.float32)
        up = jnp.dot(x, w_up, preferred_element_type=jnp.float32)
        hidden = (jax.nn.gelu(gate) * up).astype(jnp.bfloat16)
        term = jnp.dot(hidden, w_down, preferred_element_type=jnp.float32).astype(jnp.bfloat16)
        return lax.psum(term, "tp")

    return jax.shard_map(
        step,
        mesh=mesh,
        in_specs=(P("dp", None), P(None, "tp"), P(None, "tp"), P("tp", None)),
        out_specs=P("dp", None),
        check_vma=False,
    )
```

profile of v0, /device:TPU:0, one launch (start us, length us, event | category | flops | bytes accessed | tf_op | source)
XLA Modules:
  0.0 76.9 jit_solution(6935667425730077900)
XLA Ops:
  6.5 0.0 copy-start
  6.5 0.0 all-reduce.2.cloned.1.call-start
  6.5 1.2 %copy-done = bf16[128,4096]{1,0:T(8,128)(2,1)S(1)} copy-done((bf16[128,4096]{1,0:T(8,128)(2,1)S(1)}, bf16[128,4096]{1,0:T(8,128)(2,1)}, u32[]{:S(2)}) %copy-start) | copy-done | bytes 1048600
  7.8 8.5 %fusion.8 = f32[128,2560]{1,0:T(8,128)S(1)} fusion(bf16[128,4096]{1,0:T(8,128)(2,1)S(1)} %copy-done, bf16[4096,2560]{1,0:T(8,128)(2,1)} %param.5), kind=kOutput, calls=%fused_computation.11 | convolution fusion | flops 2684354560 | bytes 23330816 | tf_op jit(solution)/shard_map/dot_general | solution.py:9
  16.3 17.6 %convolution_convert_fusion = bf16[128,4096]{1,0:T(8,128)(2,1)} fusion(bf16[2560,4096]{1,0:T(8,128)(2,1)} %param.7, bf16[128,4096]{1,0:T(8,128)(2,1)S(1)} %copy-done, bf16[4096,2560]{1,0:T(8,128)(2,1)} %param.6, f32[128,2560]{1,0:T(8,128)S(1)} %fusion.8), kind=kOutput, calls=%fused_computation | convolution fusion | flops 5372510208 | bytes 45350912 | tf_op jit(solution)/shard_map/dot_general | solution.py:12
  33.9 0.0 all-reduce.2.cloned.1.call-update
  33.9 0.0 copy-start.1
  34.0 33.8 %all-reduce.2.cloned.1.call-done = bf16[128,4096]{1,0:T(8,128)(2,1)} async-done(((bf16[128,4096]{1,0:T(8,128)(2,1)}), bf16[128,4096]{1,0:T(8,128)(2,1)}) %all-reduce.2.cloned.1.call-update) | async-done | bytes 1048592 | tf_op jit(solution)/shard_map/psum | solution.py:13
  67.7 2.3 %copy.6 = bf16[128,4096]{1,0:T(8,128)(2,1)} copy(bf16[128,4096]{1,0:T(8,128)(2,1)} %all-reduce.2.cloned.1.call-done) | data formatting | bytes 2097152
  70.0 0.0 copy-done.1
Async XLA Ops:
  6.5 1.2 %copy-start = (bf16[128,4096]{1,0:T(8,128)(2,1)S(1)}, bf16[128,4096]{1,0:T(8,128)(2,1)}, u32[]{:S(2)}) copy-start(bf16[128,4096]{1,0:T(8,128)(2,1)} %param.4) | copy-start | bytes 3145732
  6.5 61.2 %all-reduce.2.cloned.1.call-start = ((), (), s32[]{:S(2)}) async-start(), calls=%async_computation | async-start | bytes 2097152 | tf_op jit(solution)/shard_map/psum | solution.py:13
  33.9 36.1 %copy-start.1 = (bf16[128,4096]{1,0:T(8,128)(2,1)S(1)}, bf16[128,4096]{1,0:T(8,128)(2,1)}, u32[]{:S(2)}) copy-start(bf16[128,4096]{1,0:T(8,128)(2,1)} %param.4) | copy-start | bytes 3145732
Sparse Core Ops, SparseCore 0:
  34.1 33.6 all-reduce.1
where the time goes:
time: 77 us; the launch traced here: 76.9 us
  waiting for transfers between devices  33.8 us (44%)
  matrix products  26.1 us (34%)
  between operations  13.4 us (17%)
  local copies, waits for them, and re-layouts  3.52 us (5%)
    psum x1, waiting for transfers between devices, step(): return lax.psum(term, 'tp')  33.8 us
    dot_general x1, matrix products, step(): jnp.dot(hidden, w_down, preferred_element_type=jnp.float32)  17.6 us
    dot_general x1, matrix products, step(): gate = jnp.dot(x, w_gate, preferred_element_type=jnp.float32)  8.51 us
    unnamed x5, local copies, waits for them, and re-layouts  3.52 us
  transfers between devices with their start and end apart: 1, of which 1 were waited for; matrix products, arithmetic and copies ran while one was open for 0% of the time, Pallas kernels for 0%

commit v1 on v0

v1 whole, which is shorter than its diff:
```python
import functools

import jax
import jax.numpy as jnp
from jax import lax
from jax.experimental import pallas as pl
from jax.experimental.pallas import tpu as pltpu
from jax.sharding import PartitionSpec as P

MESH = pl.DeviceIdType.MESH
BF16 = jnp.bfloat16
F32 = jnp.float32

B1 = 256
KQ = 4
RING = 4
B2 = 256
LAG = 3


def kernel(
    x_hbm, wg_hbm, wu_hbm, wd_hbm, y_ref,
    xv, wgv, wuv, wdv, hid, term, pair_out, pair_in, chip_out, chip_in,
    x_sem, g_sem, u_sem, d_sem,
    ps_sem, pr_sem, cs_sem, cr_sem, ys_sem, yr_sem,
):
    rows, depth = xv.shape
    half = rows // 2
    kq = depth // KQ
    n1 = wg_hbm.shape[1] // B1
    n2 = wd_hbm.shape[1] // B2

    me = lax.axis_index("tp")
    core = lax.rem(me, 2)
    sibling = me + 1 - 2 * core
    across = lax.rem(me + 2, 4)
    mine = pl.multiple_of(core * half, half)
    theirs = pl.multiple_of((1 - core) * half, half)

    def x_copy(q):
        cols = pl.ds(q * kq, kq)
        return pltpu.make_async_copy(x_hbm.at[:, cols], xv.at[:, cols], x_sem.at[q])

    def up_copies(step, q):
        slot = lax.rem(step, RING)
        ks = pl.ds(q * kq, kq)
        cols = pl.ds(pl.multiple_of(step * B1, B1), B1)
        return (
            pltpu.make_async_copy(wg_hbm.at[ks, cols], wgv.at[slot, ks], g_sem.at[slot, q]),
            pltpu.make_async_copy(wu_hbm.at[ks, cols], wuv.at[slot, ks], u_sem.at[slot, q]),
        )

    def down_copy(j):
        cols = pl.ds(pl.multiple_of(j * B2, B2), B2)
        return pltpu.make_async_copy(wd_hbm.at[:, cols], wdv.at[j], d_sem.at[j])

    def pair_copy(j):
        return pltpu.make_async_remote_copy(
            src_ref=pair_out.at[j], dst_ref=pair_in.at[j],
            send_sem=ps_sem.at[j], recv_sem=pr_sem.at[j],
            device_id={"tp": sibling}, device_id_type=MESH,
        )

    def chip_copy(j):
        return pltpu.make_async_remote_copy(
            src_ref=chip_out.at[j], dst_ref=chip_in.at[j],
            send_sem=cs_sem.at[j], recv_sem=cr_sem.at[j],
            device_id={"tp": across}, device_id_type=MESH,
        )

    def y_copy(j):
        part = y_ref.at[pl.ds(mine, half), pl.ds(pl.multiple_of(j * B2, B2), B2)]
        return pltpu.make_async_remote_copy(
            src_ref=part, dst_ref=part,
            send_sem=ys_sem.at[j], recv_sem=yr_sem.at[j],
            device_id={"tp": sibling}, device_id_type=MESH,
        )

    for q in range(KQ):
        x_copy(q).start()
        for c in up_copies(0, q):
            c.start()
    for s in range(1, RING):
        for q in range(KQ):
            for c in up_copies(s, q):
                c.start()

    barrier = pltpu.get_barrier_semaphore()
    for peer in (sibling, across):
        pl.semaphore_signal(barrier, inc=1, device_id={"tp": peer}, device_id_type=MESH)

    def up_step(step, _):
        slot = lax.rem(step, RING)
        gate = up = None
        for q in range(KQ):
            @pl.when(step == 0)
            def _():
                x_copy(q).wait()

            for c in up_copies(step, q):
                c.wait()
            ks = pl.ds(q * kq, kq)
            g = jnp.dot(xv[:, ks], wgv[slot, ks], preferred_element_type=F32)
            u = jnp.dot(xv[:, ks], wuv[slot, ks], preferred_element_type=F32)
            gate = g if gate is None else gate + g
            up = u if up is None else up + u

        @pl.when(step + RING < n1)
        def _():
            for q in range(KQ):
                for c in up_copies(step + RING, q):
                    c.start()

        @pl.when(step + RING >= n1)
        def _():
            for i in range(n2 // RING):
                down_copy((step + RING - n1) * (n2 // RING) + i).start()

        cols = pl.ds(pl.multiple_of(step * B1, B1), B1)
        hid[:, cols] = (jax.nn.gelu(gate) * up).astype(BF16)
        return 0

    lax.fori_loop(0, n1, up_step, 0)
    pl.semaphore_wait(barrier, 2)

    def add_pair(j):
        pair_copy(j).wait_recv()
        total = term[j, pl.ds(mine, half), :] + pair_in[j].astype(F32)
        chip_out[j] = total.astype(BF16)
        chip_copy(j).start()

    def down_step(j, _):
        down_copy(j).wait()
        term[j] = jnp.dot(hid[...], wdv[j], preferred_element_type=F32)
        pair_out[j] = term[j, pl.ds(theirs, half), :].astype(BF16)
        pair_copy(j).start()

        @pl.when(j >= LAG)
        def _():
            add_pair(j - LAG)

        return 0

    lax.fori_loop(0, n2, down_step, 0)

    def rest_step(j, _):
        add_pair(j)
        return 0

    lax.fori_loop(n2 - LAG, n2, rest_step, 0)

    def y_step(j, _):
        chip_copy(j).wait_recv()
        total = chip_out[j].astype(F32) + chip_in[j].astype(F32)
        cols = pl.ds(pl.multiple_of(j * B2, B2), B2)
        y_ref[pl.ds(mine, half), cols] = total.astype(BF16)
        y_copy(j).start()
        return 0

    lax.fori_loop(0, n2, y_step, 0)

    def end_step(j, _):
        pair_copy(j).wait_send()
        chip_copy(j).wait_send()
        y_copy(j).wait()
        return 0

    lax.fori_loop(0, n2, end_step, 0)


def solution(mesh):
    def step(x, w_gate, w_up, w_down):
        rows, depth = x.shape
        ff = w_gate.shape[1]
        n2 = depth // B2
        dma = pltpu.SemaphoreType.DMA
        hbm = pl.BlockSpec(memory_space=pltpu.HBM)
        return pl.pallas_call(
            kernel,
            name="mlp",
            out_shape=jax.ShapeDtypeStruct((rows, depth), BF16),
            in_specs=[hbm] * 4,
            out_specs=pl.BlockSpec(memory_space=pltpu.VMEM),
            scratch_shapes=[
                pltpu.VMEM((rows, depth), BF16),
                pltpu.VMEM((RING, depth, B1), BF16),
                pltpu.VMEM((RING, depth, B1), BF16),
                pltpu.VMEM((n2, ff, B2), BF16),
                pltpu.VMEM((rows, ff), BF16),
                pltpu.VMEM((n2, rows, B2), F32),
                pltpu.VMEM((n2, rows // 2, B2), BF16),
                pltpu.VMEM((n2, rows // 2, B2), BF16),
                pltpu.VMEM((n2, rows // 2, B2), BF16),
                pltpu.VMEM((n2, rows // 2, B2), BF16),
                dma((KQ,)), dma((RING, KQ)), dma((RING, KQ)), dma((n2,)),
                dma((n2,)), dma((n2,)), dma((n2,)), dma((n2,)), dma((n2,)), dma((n2,)),
            ],
            compiler_params=pltpu.CompilerParams(
                collective_id=0, has_side_effects=True, vmem_limit_bytes=60 * 1024 * 1024
            ),
            cost_estimate=pl.CostEstimate(
                flops=6 * rows * depth * ff, bytes_accessed=6 * depth * ff, transcendentals=rows * ff
            ),
        )(x, w_gate, w_up, w_down)

    return jax.shard_map(
        step,
        mesh=mesh,
        in_specs=(P("dp", None), P(None, "tp"), P(None, "tp"), P("tp", None)),
        out_specs=P("dp", None),
        check_vma=False,
    )
```

time: 77 us -> 37.9 us (0.49)
  Pallas kernels: 0 us -> 35.5 us
  waiting for transfers between devices: 33.8 us -> 0 us
  matrix products: 26.1 us -> 0 us
  between operations: 13.4 us -> 0.01 us
  local copies, waits for them, and re-layouts: 3.52 us -> 2.29 us
    pallas_call x0 -> x1, Pallas kernels: none -> 35.5 us  [step(): pl.pallas_call(kernel, name='mlp', out_shape=jax.ShapeDtypeStruct((rows,...]
    psum x1 -> x0, waiting for transfers between devices: 33.8 us -> none  [step(): return lax.psum(term, 'tp')]
    dot_general x2 -> x0, matrix products: 26.1 us -> none  [the longest x1 17.6 us: step(): jnp.dot(hidden, w_down, preferred_element_type=jnp.float32)]
    unnamed x5 -> x1, local copies, waits for them, and re-layouts: 3.52 us -> 2.29 us
  transfers between devices with their start and end apart: 1 -> 0, of which waited for: 1 -> 0; matrix products, arithmetic and copies ran while one was open for 0% -> 0% of each run, Pallas kernels for 0% -> 0%
where the time goes in v1:
time: 37.9 us; the launch traced here: 37.8 us
  Pallas kernels  35.5 us (94%)
  local copies, waits for them, and re-layouts  2.29 us (6%)
    pallas_call x1, Pallas kernels, step(): pl.pallas_call(kernel, name='mlp', out_shape=jax.ShapeDtypeStruct((rows,...  35.5 us
    unnamed x1, local copies, waits for them, and re-layouts  2.29 us

profile of v1, /device:TPU:0, one launch (start us, length us, event | category | flops | bytes accessed | tf_op | source)
XLA Modules:
  0.0 37.8 jit_solution(11264944130193036)
XLA Ops:
  0.0 35.5 %mlp.1 = bf16[128,4096]{1,0:T(8,128)(2,1)} custom-call(bf16[128,4096]{1,0:T(8,128)(2,1)} %x_hbm.1, bf16[4096,2560]{1,0:T(8,128)(2,1)} %wg_hbm.1, bf16[4096,2560]{1,0:T(8,128)(2,1)} %wu_hbm.1, bf16[2560,4096]{1,0:T(8,128)(2,1)} %wd_hbm.1), custom_call_target="tpu_custom_call" | custom-call | flops 8053063680 | bytes 62914560 | tf_op jit(solution)/shard_map/mlp/pallas_call | solution.py:178
  35.5 2.3 %copy.6 = bf16[128,4096]{1,0:T(8,128)(2,1)} copy(bf16[128,4096]{1,0:T(8,128)(2,1)} %mlp.1) | data formatting | bytes 2097152

commit v2 on v1

v2 whole, which is shorter than its diff:
```python
import jax
import jax.numpy as jnp
from jax import lax
from jax.experimental import pallas as pl
from jax.experimental.pallas import tpu as pltpu
from jax.sharding import PartitionSpec as P

MESH = pl.DeviceIdType.MESH
BF16 = jnp.bfloat16
F32 = jnp.float32

B1 = 256
RING = 4
LAST = 4
B2 = 256
WINDOW = 4
LAG = 2
PAIRS = 8


def kernel(
    x_hbm, wg_hbm, wu_hbm, wd_hbm, y_ref,
    xv, wgv, wuv, wdv, hid, term, pair_out, pair_in, chip_out, chip_in,
    x_sem, g_sem, u_sem, gl_sem, ul_sem, d_sem, pr_sem, cr_sem, yr_sem, send_sem,
):
    rows, depth = xv.shape
    half = rows // 2
    piece = depth // LAST
    n1 = wg_hbm.shape[1] // B1
    n2 = wd_hbm.shape[1] // B2

    me = lax.axis_index("tp")
    core = lax.rem(me, 2)
    sibling = me + 1 - 2 * core
    across = lax.rem(me + 2, 4)
    mine = pl.multiple_of(core * half, half)
    theirs = pl.multiple_of((1 - core) * half, half)

    x_copy = pltpu.make_async_copy(x_hbm, xv, x_sem)

    def up_copies(step):
        slot = lax.rem(step, RING)
        cols = pl.ds(pl.multiple_of(step * B1, B1), B1)
        return (
            pltpu.make_async_copy(wg_hbm.at[:, cols], wgv.at[slot], g_sem.at[slot]),
            pltpu.make_async_copy(wu_hbm.at[:, cols], wuv.at[slot], u_sem.at[slot]),
        )

    def last_copies(q):
        slot = (n1 - 1) % RING
        ks = pl.ds(q * piece, piece)
        cols = pl.ds((n1 - 1) * B1, B1)
        return (
            pltpu.make_async_copy(wg_hbm.at[ks, cols], wgv.at[slot, ks], gl_sem.at[q]),
            pltpu.make_async_copy(wu_hbm.at[ks, cols], wuv.at[slot, ks], ul_sem.at[q]),
        )

    def down_copy(j):
        cols = pl.ds(pl.multiple_of(j * B2, B2), B2)
        return pltpu.make_async_copy(wd_hbm.at[:, cols], wdv.at[j], d_sem.at[lax.rem(j, WINDOW)])

    def pair_copy(j):
        return pltpu.make_async_remote_copy(
            src_ref=pair_out.at[j], dst_ref=pair_in.at[j],
            send_sem=send_sem.at[0], recv_sem=pr_sem.at[lax.rem(j, PAIRS)],
            device_id={"tp": sibling}, device_id_type=MESH,
        )

    def chip_copy(j):
        return pltpu.make_async_remote_copy(
            src_ref=chip_out.at[j], dst_ref=chip_in.at[j],
            send_sem=send_sem.at[1], recv_sem=cr_sem.at[j],
            device_id={"tp": across}, device_id_type=MESH,
        )

    def y_copy(j):
        part = y_ref.at[pl.ds(mine, half), pl.ds(pl.multiple_of(j * B2, B2), B2)]
        return pltpu.make_async_remote_copy(
            src_ref=part, dst_ref=part,
            send_sem=send_sem.at[2], recv_sem=yr_sem,
            device_id={"tp": sibling}, device_id_type=MESH,
        )

    x_copy.start()
    for s in range(RING):
        for c in up_copies(s):
            c.start()

    barrier = pltpu.get_barrier_semaphore()
    for peer in (sibling, across):
        pl.semaphore_signal(barrier, inc=1, device_id={"tp": peer}, device_id_type=MESH)

    x_copy.wait()

    def up_step(step, _):
        slot = lax.rem(step, RING)
        for c in up_copies(step):
            c.wait()
        gate = jnp.dot(xv[...], wgv[slot], preferred_element_type=F32)
        up = jnp.dot(xv[...], wuv[slot], preferred_element_type=F32)

        @pl.when(step + RING < n1 - 1)
        def _():
            for c in up_copies(step + RING):
                c.start()

        @pl.when(step + RING == n1 - 1)
        def _():
            for q in range(LAST):
                for c in last_copies(q):
                    c.start()
            for j in range(WINDOW):
                down_copy(j).start(priority=1)

        cols = pl.ds(pl.multiple_of(step * B1, B1), B1)
        hid[:, cols] = (jax.nn.gelu(gate) * up).astype(BF16)
        return 0

    lax.fori_loop(0, n1 - 1, up_step, 0)

    slot = (n1 - 1) % RING
    gate = up = None
    for q in range(LAST):
        for c in last_copies(q):
            c.wait()
        ks = pl.ds(q * piece, piece)
        g = jnp.dot(xv[:, ks], wgv[slot, ks], preferred_element_type=F32)
        u = jnp.dot(xv[:, ks], wuv[slot, ks], preferred_element_type=F32)
        gate = g if gate is None else gate + g
        up = u if up is None else up + u
    hid[:, pl.ds((n1 - 1) * B1, B1)] = (jax.nn.gelu(gate) * up).astype(BF16)

    pl.semaphore_wait(barrier, 2)

    def add_pair(j):
        pair_copy(j).wait_recv()
        total = term[j, pl.ds(mine, half), :] + pair_in[j].astype(F32)
        chip_out[j] = total.astype(BF16)
        chip_copy(j).start()

    def down_step(j, _):
        down_copy(j).wait()

        @pl.when(j + WINDOW < n2)
        def _():
            down_copy(j + WINDOW).start(priority=1)

        term[j] = jnp.dot(hid[...], wdv[j], preferred_element_type=F32)
        pair_out[j] = term[j, pl.ds(theirs, half), :].astype(BF16)
        pair_copy(j).start()

        @pl.when(j >= LAG)
        def _():
            add_pair(j - LAG)

        return 0

    lax.fori_loop(0, n2, down_step, 0)

    def rest_step(j, _):
        add_pair(j)
        return 0

    lax.fori_loop(n2 - LAG, n2, rest_step, 0)

    def y_step(j, _):
        chip_copy(j).wait_recv()
        total = chip_out[j].astype(F32) + chip_in[j].astype(F32)
        cols = pl.ds(pl.multiple_of(j * B2, B2), B2)
        y_ref[pl.ds(mine, half), cols] = total.astype(BF16)
        y_copy(j).start()
        return 0

    lax.fori_loop(0, n2, y_step, 0)

    pltpu.make_async_copy(pair_out, pair_out, send_sem.at[0]).wait()
    pltpu.make_async_copy(chip_out, chip_out, send_sem.at[1]).wait()
    own = y_ref.at[pl.ds(mine, half)]
    pltpu.make_async_copy(own, own, send_sem.at[2]).wait()
    other = y_ref.at[pl.ds(theirs, half)]
    pltpu.make_async_copy(other, other, yr_sem).wait()


def solution(mesh):
    def step(x, w_gate, w_up, w_down):
        rows, depth = x.shape
        ff = w_gate.shape[1]
        n2 = depth // B2
        dma = pltpu.SemaphoreType.DMA
        hbm = pl.BlockSpec(memory_space=pltpu.HBM)
        return pl.pallas_call(
            kernel,
            name="mlp",
            out_shape=pltpu.VMEM((rows, depth), BF16),
            in_specs=[hbm] * 4,
            out_specs=pl.BlockSpec(memory_space=pltpu.VMEM),
            scratch_shapes=[
                pltpu.VMEM((rows, depth), BF16),
                pltpu.VMEM((RING, depth, B1), BF16),
                pltpu.VMEM((RING, depth, B1), BF16),
                pltpu.VMEM((n2, ff, B2), BF16),
                pltpu.VMEM((rows, ff), BF16),
                pltpu.VMEM((n2, rows, B2), F32),
                pltpu.VMEM((n2, rows // 2, B2), BF16),
                pltpu.VMEM((n2, rows // 2, B2), BF16),
                pltpu.VMEM((n2, rows // 2, B2), BF16),
                pltpu.VMEM((n2, rows // 2, B2), BF16),
                dma, dma((RING,)), dma((RING,)), dma((LAST,)), dma((LAST,)), dma((WINDOW,)),
                dma((PAIRS,)), dma((n2,)), dma, dma((3,)),
            ],
            compiler_params=pltpu.CompilerParams(
                collective_id=0, has_side_effects=True, vmem_limit_bytes=60 * 1024 * 1024
            ),
            cost_estimate=pl.CostEstimate(
                flops=6 * rows * depth * ff, bytes_accessed=6 * depth * ff, transcendentals=rows * ff
            ),
        )(x, w_gate, w_up, w_down)

    return jax.shard_map(
        step,
        mesh=mesh,
        in_specs=(P("dp", None), P(None, "tp"), P(None, "tp"), P("tp", None)),
        out_specs=P("dp", None),
        check_vma=False,
    )
```

time: 37.9 us -> 33.9 us (0.89)
  Pallas kernels: 35.5 us -> 32.8 us
  local copies, waits for them, and re-layouts: 2.29 us -> 0.97 us
    pallas_call x1, Pallas kernels: 35.5 us -> 32.8 us  [step(): pl.pallas_call(kernel, name='mlp', out_shape=pltpu.VMEM((rows, depth), BF...]
    unnamed x1, local copies, waits for them, and re-layouts: 2.29 us -> 0.97 us
where the time goes in v2:
time: 33.9 us; the launch traced here: 33.8 us
  Pallas kernels  32.8 us (97%)
  local copies, waits for them, and re-layouts  0.97 us (3%)
    pallas_call x1, Pallas kernels, step(): pl.pallas_call(kernel, name='mlp', out_shape=pltpu.VMEM((rows, depth), BF...  32.8 us
    unnamed x1, local copies, waits for them, and re-layouts  0.97 us

profile of v2, /device:TPU:0, one launch (start us, length us, event | category | flops | bytes accessed | tf_op | source)
XLA Modules:
  0.0 33.8 jit_solution(1432717915088107553)
XLA Ops:
  0.0 32.8 %mlp.1 = bf16[128,4096]{1,0:T(8,128)(2,1)S(1)} custom-call(bf16[128,4096]{1,0:T(8,128)(2,1)} %x_hbm.1, bf16[4096,2560]{1,0:T(8,128)(2,1)} %wg_hbm.1, bf16[4096,2560]{1,0:T(8,128)(2,1)} %wu_hbm.1, bf16[2560,4096]{1,0:T(8,128)(2,1)} %wd_hbm.1), custom_call_target="tpu_custom_call" | custom-call | flops 8053063680 | bytes 62914560 | tf_op jit(solution)/shard_map/mlp/pallas_call | solution.py:191
  32.9 1.0 %copy.6 = bf16[128,4096]{1,0:T(8,128)(2,1)} copy(bf16[128,4096]{1,0:T(8,128)(2,1)S(1)} %mlp.1) | data formatting | bytes 2097152
